TPU v7x, 32 devices: a whole 2x2x4 slice. The times are simulated.
32 devices in a mesh: depth: 8 (over y, x, core), rays: 4 (over z).
Axes of the slice: x: 2, y: 2, z: 4, core: 2. Of those that a mesh axis runs over, the one named last changes fastest.
Arguments:
- density: float32 [256, 65536], P('depth', 'rays'), may hold values from 0.0001953125 to 0.815625
- radiance: float32 [3, 256, 65536], P(None, 'depth', 'rays'), may hold values from 0 to 1
- target: float32 [3, 65536], P(None, 'rays'), may hold values from 0 to 1
Outputs:
- grad_density: float32 [256, 65536], P('depth', 'rays')
- loss_mean: float32 [], replicated
All inputs are finite; a program needn't handle non-finite values.
Results may differ from a plain program's by a relative error of at most 0.0003.
Values sent between devices are 32-bit elements; how exact they have to be, the bound alone decides.
A program may use at most 128 MiB of HBM per device.

v0:
```python
import jax
import jax.numpy as jnp
from jax import lax
from jax.sharding import PartitionSpec as P


def shifted(value, axis, steps):
    count = lax.axis_size(axis)
    initial, last = (max(0, -steps), min(count, count - steps))
    return lax.ppermute(value, axis, [(source, source + steps) for source in range(initial, last)])


def on_device(density, radiance, target):
    ray_count = density.shape[1]
    rim_density, rim_color = shifted((density[:1], radiance[:, :1]), "depth", -1)
    sample_density = 0.5 * (density + jnp.concatenate([density[1:], rim_density], axis=0))
    sample_color = 0.5 * (radiance + jnp.concatenate([radiance[:, 1:], rim_color], axis=1))
    opacity = -jnp.expm1(-sample_density)
    zero_row = jnp.zeros((1, ray_count), jnp.float32)
    running = jnp.cumsum(sample_density, axis=0)
    optical = jnp.concatenate([zero_row, running[:-1]], axis=0)
    slab_depth = running[-1]
    local_transmit = jnp.exp(-optical)
    emitted = (local_transmit * opacity)[None] * sample_color
    color_prefix = jnp.cumsum(emitted, axis=1)
    slab_color = color_prefix[:, -1]
    stacked = jnp.concatenate([slab_depth[None], slab_color], axis=0)[None]
    all_slabs = lax.all_gather(stacked, "depth", axis=0, tiled=True)
    depths = all_slabs[:, 0]
    depth_running = jnp.cumsum(depths, axis=0)
    starts = jnp.concatenate([zero_row, depth_running[:-1]], axis=0)
    weighted = jnp.exp(-starts)[:, None, :] * all_slabs[:, 1:]
    slab_number = jnp.arange(all_slabs.shape[0], dtype=jnp.int32)
    earlier_mask = slab_number < lax.axis_index("depth")
    start_depth = jnp.sum(jnp.where(earlier_mask[:, None], depths, 0.0), axis=0)
    color_before = jnp.sum(jnp.where(earlier_mask[:, None, None], weighted, 0.0), axis=0)
    pixel_color = jnp.sum(weighted, axis=0)
    offset = jnp.exp(-start_depth)
    transmit = offset[None] * local_transmit
    remaining = (
        pixel_color[:, None, :] - color_before[:, None, :] - offset[None, None, :] * color_prefix
    )
    residual_grad = 2.0 * (pixel_color - target)
    transmit_next = transmit * jnp.exp(-sample_density)
    bracket = transmit_next[None] * sample_color - remaining
    sample_grad = jnp.sum(residual_grad[:, None, :] * bracket, axis=0)
    previous = shifted(sample_grad[-1:], "depth", 1)
    grad_density = 0.5 * (sample_grad + jnp.concatenate([previous, sample_grad[:-1]], axis=0))
    error_term = pixel_color - target
    loss_part = jnp.sum(error_term * error_term)
    total_rays = ray_count * lax.axis_size("rays")
    loss_mean = lax.psum(loss_part, "rays") / (3.0 * total_rays)
    return (grad_density, loss_mean)


def solution(mesh):
    in_specs = (P("depth", "rays"), P(None, "depth", "rays"), P(None, "rays"))
    out_specs = (P("depth", "rays"), P())
    return jax.shard_map(
        on_device, mesh=mesh, in_specs=in_specs, out_specs=out_specs, check_vma=False
    )
```

profile of v0, /device:TPU:0, one launch (start us, length us, event | category | flops | bytes accessed | tf_op | source)
XLA Modules:
  0.0 120.2 jit_solution(12348934080758877961)
XLA Ops:
  7.2 0.0 all-gather.4.cloned.1.call-start
  7.2 1.1 slice.37
  8.3 1.3 %collective-permute-start = (f32[1,16384]{1,0:T(1,128)S(1)}, f32[1,16384]{1,0:T(1,128)S(1)}, u32[]{:S(2)}, u32[]{:S(2)}) collective-permute-start(f32[1,16384]{1,0:T(1,128)S(1)} %slice.37), channel_id=1, source_target_pairs={{4,0},{8,4},{12,8},{16,12},{20,16},{24,20},{28,24},{5,1},{9,5},{13... | collective-permute-start | bytes 196616 | tf_op jit(solution)/shard_map/ppermute | solution.py:10
  9.6 1.5 %slice.40 = f32[3,1,16384]{2,1,0:T(1,128)S(1)} slice(f32[3,32,16384]{2,1,0:T(8,128)} %param.4), slice={[0:3], [0:1], [0:16384]} | slice | bytes 393216 | tf_op jit(solution)/shard_map/slice | solution.py:15
  11.1 1.3 %collective-permute-start.1 = (f32[3,1,16384]{2,1,0:T(1,128)S(1)}, f32[3,1,16384]{2,1,0:T(1,128)S(1)}, u32[]{:S(2)}, u32[]{:S(2)}) collective-permute-start(f32[3,1,16384]{2,1,0:T(1,128)S(1)} %slice.40), channel_id=1, source_target_pairs={{4,0},{8,4},{12,8},{16,12},{20,16},{24,20},{28,24},{5,1},{9,5},{13... | collective-permute-start | bytes 589832 | tf_op jit(solution)/shard_map/ppermute | solution.py:10
  12.4 1.7 %slice.36 = f32[31,16384]{1,0:T(8,128)S(1)} slice(f32[32,16384]{1,0:T(8,128)} %param.3), slice={[1:32], [0:16384]} | slice | bytes 4063232 | tf_op jit(solution)/shard_map/slice | solution.py:16
  14.2 6.2 %slice.39 = f32[3,31,16384]{2,1,0:T(8,128)} slice(f32[3,32,16384]{2,1,0:T(8,128)} %param.4), slice={[0:3], [1:32], [0:16384]} | slice | bytes 12189696 | tf_op jit(solution)/shard_map/slice | solution.py:17
  20.4 0.3 fusion
  20.7 3.0 %reduce_window_sum.33 = f32[32,16384]{1,0:T(8,128)} reduce-window(f32[32,16384]{1,0:T(8,128)S(1)} %fusion, f32[]{:T(128)} %constant.12.clone.1), window={size=32x1 pad=31_0x0_0}, to_apply=%region_0.0 | reduce-window | flops 16252928 | bytes 4194308 | tf_op jit(solution)/shard_map/jit(cumsum)/reduce_window_sum | solution.py:20
  23.7 2.8 %multiply_multiply_fusion.1 = f32[32,16384]{1,0:T(8,128)S(1)} fusion(f32[32,16384]{1,0:T(8,128)S(1)} %fusion, f32[31,16384]{1,0:T(8,128)} %bitcast.16), kind=kLoop, calls=%fused_computation.10 | loop fusion | flops 2621440 | bytes 6225920 | tf_op jit(solution)/shard_map/mul | solution.py:24
  26.6 1.1 slice.48
  27.7 6.2 %broadcast_multiply_fusion = f32[3,32,16384]{2,1,0:T(8,128)} fusion(f32[32,16384]{1,0:T(8,128)S(1)} %multiply_multiply_fusion.1, f32[3,32,16384]{2,1,0:T(8,128)} %param.4, f32[3,1,16384]{2,1,0:T(1,128)S(1)} %collective-permute-done.1, f32[3,31,16384]{2,1,0:T(8,128)S(1)} %copy-done), kind=kLoop, calls=%fused_computation.2 | loop fusion | flops 4718592 | bytes 20971520 | tf_op jit(solution)/shard_map/mul | solution.py:24
  33.9 8.7 %reduce_window_sum.34 = f32[3,32,16384]{2,1,0:T(8,128)} reduce-window(f32[3,32,16384]{2,1,0:T(8,128)} %broadcast_multiply_fusion, f32[]{:T(128)} %constant.12.clone.1), window={size=1x32x1 pad=0_0x31_0x0_0}, to_apply=%region_1.2 | reduce-window | flops 48758784 | bytes 12582916 | tf_op jit(solution)/shard_map/jit(cumsum)/reduce_window_sum | solution.py:25
  42.6 1.6 %slice.50 = f32[3,1,16384]{2,1,0:T(1,128)S(1)} slice(f32[3,32,16384]{2,1,0:T(8,128)} %reduce_window_sum.34), slice={[0:3], [31:32], [0:16384]} | slice | bytes 393216 | tf_op jit(solution)/shard_map/slice | solution.py:26
  44.2 0.1 copy.12
  44.3 0.8 maximum_bitcast_fusion
  45.1 0.0 all-gather.4.cloned.1.call-update
  45.2 32.5 %all-gather.4.cloned.1.call-done = f32[8,4,16384]{2,1,0:T(4,128)} async-done(((f32[1,4,16384]{2,1,0:T(4,128)}), f32[8,4,16384]{2,1,0:T(4,128)}) %all-gather.4.cloned.1.call-update) | async-done | bytes 2097168 | tf_op jit(solution)/shard_map/all_gather | solution.py:28
  77.7 2.0 %slice.51 = f32[8,1,16384]{2,1,0:T(1,128)S(1)} slice(f32[8,4,16384]{2,1,0:T(4,128)} %all-gather.4.cloned.1.call-done), slice={[0:8], [0:1], [0:16384]} | slice | bytes 1048576 | tf_op jit(solution)/shard_map/slice | solution.py:29
  79.7 1.1 copy.11
  80.8 1.5 %reduce_window_sum.35 = f32[8,16384]{1,0:T(8,128)S(1)} reduce-window(f32[8,16384]{1,0:T(8,128)} %bitcast.19, f32[]{:T(128)} %constant.12.clone.1), window={size=8x1 pad=7_0x0_0}, to_apply=%region_2.3 | reduce-window | flops 917504 | bytes 1048580 | tf_op jit(solution)/shard_map/jit(cumsum)/reduce_window_sum | solution.py:30
  82.3 0.1 negate_exponential_fusion.1
  82.4 0.4 select_reduce_fusion.1
  82.9 0.0 slice-start.1
  82.9 2.5 %multiply_multiply_fusion = f32[32,16384]{1,0:T(8,128)S(1)} fusion(f32[32,16384]{1,0:T(8,128)S(1)} %fusion, f32[31,16384]{1,0:T(8,128)} %bitcast.17, f32[16384]{0:T(1024)S(1)} %negate_exponential_fusion.2), kind=kLoop, calls=%fused_computation.9 | loop fusion | flops 2621440 | bytes 6291456 | tf_op jit(solution)/shard_map/mul | solution.py:45
  85.4 3.7 %select_reduce_fusion = (f32[3,16384]{1,0:T(4,128)S(1)}, f32[3,16384]{1,0:T(4,128)S(1)}) fusion(f32[8,4,16384]{2,1,0:T(4,128)} %all-gather.4.cloned.1.call-done, f32[8,16384]{1,0:T(8,128)S(1)} %negate_exponential_fusion.1, pred[8]{0:T(512)(128)(4,1)S(1)} %iota_compare_fusion), kind=kLoop, calls=%fused_computation.8 | loop fusion | flops 1474560 | bytes 2490376 | tf_op jit(solution)/shard_map/reduce_sum | solution.py:36
  89.1 1.7 %multiply_reduce_fusion.1 = (f32[]{:T(128)}, f32[3,16384]{1,0:T(4,128)S(1)}, f32[3,16384]{1,0:T(4,128)S(1)}) fusion(f32[3,16384]{1,0:T(4,128)S(1)} %get-tuple-element.3, f32[3,16384]{1,0:T(4,128)} %param.5, f32[3,16384]{1,0:T(4,128)S(1)} %get-tuple-element.2), kind=kLoop, calls=%fused_computation.18 | loop fusion | flops 245759 | bytes 983044 | tf_op jit(solution)/shard_map/reduce_sum | solution.py:50
  90.8 4.5 %multiply_reduce_fusion = f32[32,16384]{1,0:T(8,128)S(1)} fusion(f32[3,32,16384]{2,1,0:T(8,128)S(1)} %copy-done.1, f32[16384]{0:T(1024)S(1)} %negate_exponential_fusion.2, f32[3,16384]{1,0:T(4,128)S(1)} %get-tuple-element.6, f32[32,16384]{1,0:T(8,128)S(1)} %multiply_multiply_fusion, f32[3,16384]{1,0:T(4,128)S(1)} %get-tuple-element.5, ...), kind=kLoop, calls=%fused_computation.1 | loop fusion | flops 12058624 | bytes 23527424 | tf_op jit(solution)/shard_map/reduce_sum | solution.py:46
  95.4 0.1 slice.54
  95.4 2.1 %collective-permute-start.2 = (f32[1,16384]{1,0:T(1,128)S(1)}, f32[1,16384]{1,0:T(1,128)S(1)}, u32[]{:S(2)}, u32[]{:S(2)}) collective-permute-start(f32[1,16384]{1,0:T(1,128)S(1)} %slice.54), channel_id=1, source_target_pairs={{0,4},{4,8},{8,12},{12,16},{16,20},{20,24},{24,28},{1,5},{5,9},{9,... | collective-permute-start | bytes 196616 | tf_op jit(solution)/shard_map/ppermute | solution.py:10
  97.6 12.3 %psum.7 = f32[]{:T(128)} all-reduce(f32[]{:T(128)} %get-tuple-element.4), channel_id=1, replica_groups=mesh['depth'=8,'rays'=4] {'rays'}, use_global_device_ids=true, to_apply=%region_8.9 | all-reduce | flops 1 | bytes 8 | tf_op jit(solution)/shard_map/psum | solution.py:52
  110.6 1.6 %fusion.1 = f32[32,16384]{1,0:T(8,128)} fusion(f32[32,16384]{1,0:T(8,128)S(1)} %multiply_reduce_fusion, f32[31,16384]{1,0:T(8,128)S(1)} %bitcast.15, f32[1,16384]{1,0:T(1,128)S(1)} %collective-permute-done.2), kind=kLoop, calls=%fused_computation.7 | loop fusion | flops 1572864 | bytes 6291456 | tf_op jit(solution)/shard_map/mul | solution.py:48
  (15 shorter events, 0.1 us)
Async XLA Ops:
  7.2 70.5 %all-gather.4.cloned.1.call-start = ((), (), s32[]{:S(2)}) async-start(), calls=%async_computation | async-start | bytes 2359296 | tf_op jit(solution)/shard_map/all_gather | solution.py:28
  8.3 12.1 %collective-permute-start = (f32[1,16384]{1,0:T(1,128)S(1)}, f32[1,16384]{1,0:T(1,128)S(1)}, u32[]{:S(2)}, u32[]{:S(2)}) collective-permute-start(f32[1,16384]{1,0:T(1,128)S(1)} %slice.37), channel_id=1, source_target_pairs={{4,0},{8,4},{12,8},{16,12},{20,16},{24,20},{28,24},{5,1},{9,5},{13... | collective-permute-start | bytes 196616 | tf_op jit(solution)/shard_map/ppermute | solution.py:10
  11.1 16.6 %collective-permute-start.1 = (f32[3,1,16384]{2,1,0:T(1,128)S(1)}, f32[3,1,16384]{2,1,0:T(1,128)S(1)}, u32[]{:S(2)}, u32[]{:S(2)}) collective-permute-start(f32[3,1,16384]{2,1,0:T(1,128)S(1)} %slice.40), channel_id=1, source_target_pairs={{4,0},{8,4},{12,8},{16,12},{20,16},{24,20},{28,24},{5,1},{9,5},{13... | collective-permute-start | bytes 589832 | tf_op jit(solution)/shard_map/ppermute | solution.py:10
  14.2 6.2 %copy-start.2 = (f32[32,16384]{1,0:T(8,128)S(1)}, f32[32,16384]{1,0:T(8,128)}, u32[]{:S(2)}) copy-start(f32[32,16384]{1,0:T(8,128)} %param.3) | copy-start | bytes 6291460
  23.7 4.0 %copy-start = (f32[3,31,16384]{2,1,0:T(8,128)S(1)}, f32[3,31,16384]{2,1,0:T(8,128)}, u32[]{:S(2)}) copy-start(f32[3,31,16384]{2,1,0:T(8,128)} %slice.39) | copy-start | bytes 18284548
  82.3 8.5 %copy-start.1 = (f32[3,32,16384]{2,1,0:T(8,128)S(1)}, f32[3,32,16384]{2,1,0:T(8,128)}, u32[]{:S(2)}) copy-start(f32[3,32,16384]{2,1,0:T(8,128)} %reduce_window_sum.34) | copy-start | bytes 18874372
  82.4 8.4 %slice-start = ((s8[6291456]{0:T(1024)(128)(4,1)}), s8[4194304]{0:T(1024)(128)(4,1)S(1)}, s32[]{:S(2)}) async-start(s8[6291456]{0:T(1024)(128)(4,1)} %bitcast.13), calls=%async_computation.1 | async-start | bytes 8388608
  82.9 7.9 %slice-start.1 = ((s8[6291456]{0:T(1024)(128)(4,1)}), s8[2097152]{0:T(1024)(128)(4,1)S(1)}, s32[]{:S(2)}) async-start(s8[6291456]{0:T(1024)(128)(4,1)} %bitcast.13), calls=%async_computation.2 | async-start | bytes 4194304
  95.4 15.1 %collective-permute-start.2 = (f32[1,16384]{1,0:T(1,128)S(1)}, f32[1,16384]{1,0:T(1,128)S(1)}, u32[]{:S(2)}, u32[]{:S(2)}) collective-permute-start(f32[1,16384]{1,0:T(1,128)S(1)} %slice.54), channel_id=1, source_target_pairs={{0,4},{4,8},{8,12},{12,16},{16,20},{20,24},{24,28},{1,5},{5,9},{9,... | collective-permute-start | bytes 196616 | tf_op jit(solution)/shard_map/ppermute | solution.py:10
Sparse Core Ops, SparseCore 0:
  45.3 32.3 all-gather.3
where the time goes:
time: 121 us; the launch traced here: 120 us
  other arithmetic  38 us (31%)
  waiting for transfers between devices  32.5 us (27%)
  local copies, waits for them, and re-layouts  16.5 us (14%)
  between operations  16 us (13%)
  blocking collectives  12.3 us (10%)
  starting transfers between devices  4.76 us (4%)
    all_gather x1, waiting for transfers between devices, on_device(): all_slabs = lax.all_gather(stacked, 'depth', axis=0, tiled=True)  32.5 us
    psum x1, blocking collectives, on_device(): loss_mean = lax.psum(loss_part, 'rays') / (3.0 * total_rays)  12.3 us
    mul x2, other arithmetic, on_device(): emitted = (local_transmit * opacity)[None] * sample_color  9.08 us
    another operation x1, other arithmetic, on_device(): color_prefix = jnp.cumsum(emitted, axis=1)  8.66 us
    slice x1, local copies, waits for them, and re-layouts, on_device(): radiance[:, 1:]  6.22 us
    ppermute x3, starting transfers between devices, shifted(): lax.ppermute(value, axis, [(source, source + steps) for source in range(i...  4.73 us
    reduce_sum x1, other arithmetic, on_device(): sample_grad = jnp.sum(residual_grad[:, None, :] * bracket, axis=0)  4.55 us
    reduce_sum x1, other arithmetic, on_device(): jnp.sum(jnp.where(earlier_mask[:, None, None], weighted, 0.0), axis=0)  3.69 us
  transfers between devices with their start and end apart: 4, of which 1 were waited for; matrix products, arithmetic and copies ran while one was open for 14% of the time, Pallas kernels for 0%

commit v1 on v0

v1 whole, which is shorter than its diff:
```python
import functools
import math

import jax
import jax.numpy as jnp
from jax import lax
from jax.experimental import pallas as pl
from jax.experimental.pallas import tpu as pltpu
from jax.sharding import PartitionSpec as P

MESH = pl.DeviceIdType.MESH
SUB, LANE = 8, 128
CHANNELS = 3
HALF_LOG2E = 0.5 * math.log2(math.e)


def kernel(sizes, density_hbm, radiance_hbm, target_ref, grad, loss_ref,
           dens, rad, trans, next_out, prev_out, next_in, prev_in,
           summary, gathered, before, answer, answers, loss_z, loss_sum, loss_d,
           load_sem, halo_send, halo_recv, sum_send, sum_recv,
           ans_send, ans_recv, z_send, z_recv, d_send, d_recv):
    slabs, tiles_z, rows, tiles = sizes
    bands = rows // SUB
    share = tiles // slabs
    group = min(SUB, share)
    plane = rows * tiles
    me = lax.axis_index("depth")
    my_z = lax.axis_index("rays")

    order = [0] + ([bands - 1] if bands > 1 else []) + list(range(1, bands - 1))
    span = tiles * SUB

    def load(band):
        copies = [pltpu.make_async_copy(
            density_hbm.at[pl.ds(band * span, span)], dens.at[pl.ds(band * span, span)],
            load_sem.at[0, band])]
        for c in range(CHANNELS):
            piece = pl.ds(c * plane + band * span, span)
            copies.append(pltpu.make_async_copy(
                radiance_hbm.at[piece], rad.at[piece], load_sem.at[1 + c, band]))
        return copies

    for band in order:
        for copy in load(band):
            copy.start()

    barrier = pltpu.get_barrier_semaphore()
    for k in range(1, slabs):
        pl.semaphore_signal(barrier, inc=1, device_id={"depth": lax.rem(me + k, slabs)}, device_id_type=MESH)
    for k in range(1, tiles_z):
        pl.semaphore_signal(barrier, inc=1, device_id={"rays": lax.rem(my_z + k, tiles_z)}, device_id_type=MESH)

    def row(ref, start, first, count, r):
        base = start + ((r // SUB) * tiles + first) * SUB + r % SUB
        return ref[pl.ds(base, count, stride=SUB), :]

    for band in order[:2]:
        for copy in load(band):
            copy.wait()

    @pl.loop(0, tiles // group)
    def _(b):
        first = b * group
        chunk = first // share
        inner = pl.ds(first - chunk * share, group)
        next_out[chunk, 0, inner] = row(dens, 0, first, group, 0)
        for c in range(CHANNELS):
            next_out[chunk, 1 + c, inner] = row(rad, c * plane, first, group, 0)
            prev_out[chunk, c, inner] = row(rad, c * plane, first, group, rows - 1)

    pl.semaphore_wait(barrier, slabs - 1 + tiles_z - 1)

    def halo(direction, chunk):
        if direction == 0:
            return pltpu.make_async_remote_copy(
                src_ref=next_out.at[chunk], dst_ref=next_in.at[chunk],
                send_sem=halo_send.at[0, chunk], recv_sem=halo_recv.at[0, chunk],
                device_id={"depth": lax.rem(me + slabs - 1, slabs)}, device_id_type=MESH)
        return pltpu.make_async_remote_copy(
            src_ref=prev_out.at[chunk], dst_ref=prev_in.at[chunk],
            send_sem=halo_send.at[1, chunk], recv_sem=halo_recv.at[1, chunk],
            device_id={"depth": lax.rem(me + 1, slabs)}, device_id_type=MESH)

    @pl.when(me > 0)
    def _():
        for k in range(slabs):
            halo(0, lax.rem(me + k, slabs)).start()

    @pl.when(me < slabs - 1)
    def _():
        for k in range(slabs):
            halo(1, lax.rem(me + slabs - k, slabs)).start()

    @pl.when(me == slabs - 1)
    def _():
        next_in[...] = jnp.zeros_like(next_in)

    @pl.when(me == 0)
    def _():
        prev_in[...] = jnp.zeros_like(prev_in)

    for band in order[2:]:
        for copy in load(band):
            copy.wait()

    def send_summary(q):
        return pltpu.make_async_remote_copy(
            src_ref=summary.at[q], dst_ref=gathered.at[me],
            send_sem=sum_send.at[q], recv_sem=sum_recv.at[me],
            device_id={"depth": q}, device_id_type=MESH)

    def recv_summary(q):
        return pltpu.make_async_remote_copy(
            src_ref=summary.at[q], dst_ref=gathered.at[q],
            send_sem=sum_send.at[q], recv_sem=sum_recv.at[q],
            device_id={"depth": q}, device_id_type=MESH)

    def forward(p):
        @pl.when(me < slabs - 1)
        def _():
            halo(0, p).wait_recv()

        @pl.loop(0, share // group)
        def _(b):
            inner = pl.ds(b * group, group)
            first = p * share + b * group
            d_now = row(dens, 0, first, group, 0)
            c_now = [row(rad, c * plane, first, group, 0) for c in range(CHANNELS)]
            depth = jnp.zeros((group, LANE), jnp.float32)
            t_now = jnp.ones((group, LANE), jnp.float32)
            color = [jnp.zeros((group, LANE), jnp.float32) for _ in range(CHANNELS)]
            for r in range(rows):
                if r + 1 < rows:
                    d_next = row(dens, 0, first, group, r + 1)
                    c_next = [row(rad, c * plane, first, group, r + 1) for c in range(CHANNELS)]
                else:
                    d_next = next_in[p, 0, inner]
                    c_next = [next_in[p, 1 + c, inner] for c in range(CHANNELS)]
                depth = depth + (d_now + d_next)
                t_next = jnp.exp2(depth * (-HALF_LOG2E))
                weight = t_now - t_next
                color = [color[c] + weight * (c_now[c] + c_next[c]) for c in range(CHANNELS)]
                trans[r, pl.ds(first, group)] = t_next
                d_now, c_now, t_now = d_next, c_next, t_next
            summary[p, 0, inner] = depth
            for c in range(CHANNELS):
                summary[p, 1 + c, inner] = color[c]

    @pl.loop(1, slabs)
    def _(k):
        p = lax.rem(me + k, slabs)
        forward(p)
        send_summary(p).start()

    forward(me)
    gathered[me] = summary[me]
    @pl.loop(1, slabs)
    def _(k):
        recv_summary(lax.rem(me + slabs - k, slabs)).wait_recv()

    start = jnp.zeros((share, LANE), jnp.float32)
    pixel = [jnp.zeros((share, LANE), jnp.float32) for _ in range(CHANNELS)]
    for q in range(slabs):
        offset = jnp.exp2(start * (-HALF_LOG2E))
        answer[q, 0] = 0.25 * offset
        half = 0.5 * offset
        for c in range(CHANNELS):
            before[q, c] = pixel[c]
            pixel[c] = pixel[c] + half * gathered[q, 1 + c]
        start = start + gathered[q, 0]

    residual, loss = [], jnp.zeros((share, LANE), jnp.float32)
    for c in range(CHANNELS):
        wanted = jnp.concatenate(
            [target_ref[c:c + 1, pl.ds(pl.multiple_of((me * share + t) * LANE, LANE), LANE)] for t in range(share)], axis=0)
        error = pixel[c] - wanted
        residual.append(2.0 * error)
        loss = loss + error * error

    def send_answer(q):
        return pltpu.make_async_remote_copy(
            src_ref=answer.at[q], dst_ref=answers.at[me],
            send_sem=ans_send.at[q], recv_sem=ans_recv.at[me],
            device_id={"depth": q}, device_id_type=MESH)

    def recv_answer(q):
        return pltpu.make_async_remote_copy(
            src_ref=answer.at[q], dst_ref=answers.at[q],
            send_sem=ans_send.at[q], recv_sem=ans_recv.at[q],
            device_id={"depth": q}, device_id_type=MESH)

    for k in list(range(1, slabs)) + [0]:
        q = lax.rem(me + k, slabs)
        behind = residual[0] * (pixel[0] - before[q, 0])
        for c in range(1, CHANNELS):
            behind = behind + residual[c] * (pixel[c] - before[q, c])
        answer[q, 1] = behind
        for c in range(CHANNELS):
            answer[q, 2 + c] = residual[c]
        if k:
            send_answer(q).start()
        else:
            answers[me] = answer[me]

    loss_z[my_z] = loss

    def z_copy(z, slot):
        return pltpu.make_async_remote_copy(
            src_ref=loss_z.at[my_z], dst_ref=loss_z.at[slot],
            send_sem=z_send.at[z], recv_sem=z_recv.at[slot],
            device_id={"rays": z}, device_id_type=MESH)

    def d_copy(q, slot):
        return pltpu.make_async_remote_copy(
            src_ref=loss_sum, dst_ref=loss_d.at[slot],
            send_sem=d_send.at[q], recv_sem=d_recv.at[slot],
            device_id={"depth": q}, device_id_type=MESH)

    for k in range(1, tiles_z):
        z_copy(lax.rem(my_z + k, tiles_z), my_z).start()

    def backward(p):
        @pl.when(me > 0)
        def _():
            halo(1, p).wait_recv()

        @pl.loop(0, share // group)
        def _(b):
            inner = pl.ds(b * group, group)
            first = p * share + b * group
            scale = answers[p, 0, inner]
            behind = answers[p, 1, inner]
            res = [answers[p, 2 + c, inner] for c in range(CHANNELS)]

            def mix(values):
                total = res[0] * values[0]
                for c in range(1, CHANNELS):
                    total = total + res[c] * values[c]
                return total

            v_now = mix([row(rad, c * plane, first, group, 0) for c in range(CHANNELS)])
            a_prev = v_now + mix([prev_in[p, c, inner] for c in range(CHANNELS)])
            a_prev = jnp.where(me == 0, 2.0 * behind, a_prev)
            run = None
            t_now = None
            for r in range(rows):
                if r + 1 < rows:
                    v_next = mix([row(rad, c * plane, first, group, r + 1) for c in range(CHANNELS)])
                else:
                    v_next = mix([next_in[p, 1 + c, inner] for c in range(CHANNELS)])
                u = v_now + v_next
                a = u if r == 0 else t_now * u + run
                t_now = trans[r, pl.ds(first, group)]
                run = a - t_now * u
                base = ((r // SUB) * tiles + first) * SUB + r % SUB
                grad[pl.ds(base, group, stride=SUB), :] = scale * (a + a_prev) - behind
                a_prev, v_now = a, v_next
    backward(me)
    half_way = max(1, slabs // 2)

    @pl.loop(1, half_way)
    def _(k):
        p = lax.rem(me + slabs - k, slabs)
        recv_answer(p).wait_recv()
        backward(p)

    for k in range(1, tiles_z):
        z = lax.rem(my_z + k, tiles_z)
        z_copy(z, z).wait_recv()
    total = loss_z[0]
    for z in range(1, tiles_z):
        total = total + loss_z[z]
    loss_sum[...] = total
    loss_d[me] = total
    for k in range(1, slabs):
        d_copy(lax.rem(me + k, slabs), me).start()

    @pl.loop(half_way, slabs)
    def _(k):
        p = lax.rem(me + slabs - k, slabs)
        recv_answer(p).wait_recv()
        backward(p)

    for k in range(1, slabs):
        q = lax.rem(me + k, slabs)
        d_copy(q, q).wait_recv()
    total = loss_d[0]
    for q in range(1, slabs):
        total = total + loss_d[q]
    loss_ref[0, 0] = jnp.sum(total) / (float(CHANNELS) * tiles_z * tiles * LANE)

    @pl.when(me > 0)
    def _():
        for p in range(slabs):
            halo(0, p).wait_send()

    @pl.when(me < slabs - 1)
    def _():
        for p in range(slabs):
            halo(1, p).wait_send()

    for k in range(1, slabs):
        q = lax.rem(me + k, slabs)
        send_summary(q).wait_send()
        send_answer(q).wait_send()
        d_copy(q, me).wait_send()
    for k in range(1, tiles_z):
        z_copy(lax.rem(my_z + k, tiles_z), my_z).wait_send()


def flat(x):
    lead, (rows, rays) = x.shape[:-2], x.shape[-2:]
    x = x.reshape(-1, rows // SUB, SUB, rays // LANE, LANE)
    return x.swapaxes(2, 3).reshape(-1, LANE)


def on_device(slabs, tiles_z, density, radiance, target):
    rows, rays = density.shape
    tiles = rays // LANE
    share = tiles // slabs
    vmem = lambda *shape: pltpu.VMEM(shape, jnp.float32)
    dma = lambda *shape: pltpu.SemaphoreType.DMA(shape)
    stay = pl.BlockSpec(memory_space=pltpu.HBM)
    bands = rows // SUB
    grad, loss = pl.pallas_call(
        functools.partial(kernel, (slabs, tiles_z, rows, tiles)),
        out_shape=(
            jax.ShapeDtypeStruct((rows * tiles, LANE), jnp.float32),
            jax.ShapeDtypeStruct((1, 1), jnp.float32),
        ),
        in_specs=[stay, stay, pl.BlockSpec(memory_space=pltpu.VMEM)],
        out_specs=(pl.BlockSpec(memory_space=pltpu.VMEM), pl.BlockSpec(memory_space=pltpu.SMEM)),
        scratch_shapes=[
            vmem(rows * tiles, LANE),
            vmem(CHANNELS * rows * tiles, LANE),
            vmem(rows, tiles, LANE),
            vmem(slabs, 1 + CHANNELS, share, LANE),
            vmem(slabs, CHANNELS, share, LANE),
            vmem(slabs, 1 + CHANNELS, share, LANE),
            vmem(slabs, CHANNELS, share, LANE),
            vmem(slabs, 1 + CHANNELS, share, LANE),
            vmem(slabs, 1 + CHANNELS, share, LANE),
            vmem(slabs, CHANNELS, share, LANE),
            vmem(slabs, 2 + CHANNELS, share, LANE),
            vmem(slabs, 2 + CHANNELS, share, LANE),
            vmem(tiles_z, share, LANE),
            vmem(share, LANE),
            vmem(slabs, share, LANE),
            dma(1 + CHANNELS, bands),
            dma(2, slabs), dma(2, slabs),
            dma(slabs), dma(slabs), dma(slabs), dma(slabs),
            dma(tiles_z), dma(tiles_z), dma(slabs), dma(slabs),
        ],
        compiler_params=pltpu.CompilerParams(
            collective_id=0, has_side_effects=True, vmem_limit_bytes=58 * 1024 * 1024),
    )(flat(density), flat(radiance), target)
    grad = grad.reshape(bands, tiles, SUB, LANE).swapaxes(1, 2).reshape(rows, rays)
    return grad, loss.reshape(())


def solution(mesh):
    in_specs = (P("depth", "rays"), P(None, "depth", "rays"), P(None, "rays"))
    out_specs = (P("depth", "rays"), P())
    body = functools.partial(on_device, mesh.shape["depth"], mesh.shape["rays"])
    return jax.shard_map(body, mesh=mesh, in_specs=in_specs, out_specs=out_specs, check_vma=False)
```

time: 121 us -> 31.1 us (0.26)
  other arithmetic: 38 us -> 0 us
  waiting for transfers between devices: 32.5 us -> 0 us
  Pallas kernels: 0 us -> 25.4 us
  between operations: 16 us -> 2.37 us
  local copies, waits for them, and re-layouts: 16.5 us -> 3.05 us
  blocking collectives: 12.3 us -> 0 us
  starting transfers between devices: 4.76 us -> 0 us
    all_gather x1 -> x0, waiting for transfers between devices: 32.5 us -> none  [on_device(): all_slabs = lax.all_gather(stacked, 'depth', axis=0, tiled=True)]
    pallas_call x0 -> x1, Pallas kernels: none -> 25.4 us  [on_device(): pl.pallas_call(functools.partial(kernel, (slabs, tiles_z, rows, tiles)),...]
    slice x8 -> x0, local copies, waits for them, and re-layouts: 15.2 us -> none  [the longest x1 6.22 us: on_device(): radiance[:, 1:]]
    mul x5 -> x0, other arithmetic: 13.5 us -> none  [the longest x2 9.08 us: on_device(): emitted = (local_transmit * opacity)[None] * sample_color]
    another operation x3 -> x0, other arithmetic: 13.2 us -> none  [the longest x1 8.66 us: on_device(): color_prefix = jnp.cumsum(emitted, axis=1)]
    psum x1 -> x0, blocking collectives: 12.3 us -> none  [on_device(): loss_mean = lax.psum(loss_part, 'rays') / (3.0 * total_rays)]
    reduce_sum x4 -> x0, other arithmetic: 10.4 us -> none  [the longest x1 4.55 us: on_device(): sample_grad = jnp.sum(residual_grad[:, None, :] * bracket, axis=0)]
    ppermute x3 -> x0, starting transfers between devices: 4.73 us -> none  [shifted(): lax.ppermute(value, axis, [(source, source + steps) for source in range(i...]
  transfers between devices with their start and end apart: 4 -> 0, of which waited for: 1 -> 0; matrix products, arithmetic and copies ran while one was open for 14% -> 0% of each run, Pallas kernels for 0% -> 0%
where the time goes in v1:
time: 31.1 us; the launch traced here: 30.9 us
  Pallas kernels  25.4 us (82%)
  local copies, waits for them, and re-layouts  3.05 us (10%)
  between operations  2.37 us (8%)
    pallas_call x1, Pallas kernels, on_device(): pl.pallas_call(functools.partial(kernel, (slabs, tiles_z, rows, tiles)),...  25.4 us
    unnamed x1, local copies, waits for them, and re-layouts  3.05 us

profile of v1, /device:TPU:0, one launch (start us, length us, event | category | flops | bytes accessed | tf_op | source)
XLA Modules:
  0.0 30.9 jit_solution(616386928821100172)
XLA Ops:
  0.6 25.4 %shard_map.50 = (f32[4096,128]{1,0:T(8,128)}, f32[1,1]{1,0:T(1,128)}) custom-call(f32[4096,128]{1,0:T(8,128)} %bitcast.18, f32[12288,128]{1,0:T(8,128)} %bitcast.16, f32[3,16384]{1,0:T(4,128)} %target_ref.1), custom_call_target="tpu_custom_call" | custom-call | tf_op jit(solution)/shard_map/pallas_call | solution.py:325
  26.1 3.0 %copy.7 = f32[32,16384]{1,0:T(8,128)} copy(f32[32,16384]{1,0:T(8,128)} %bitcast.17) | data formatting | bytes 4194304

commit v2 on v1

--- a/solution.py
+++ b/solution.py
@@ -14,11 +14,11 @@
 HALF_LOG2E = 0.5 * math.log2(math.e)
 
 
-def kernel(sizes, density_hbm, radiance_hbm, target_ref, grad, loss_ref,
+def kernel(sizes, density_hbm, radiance_hbm, target_hbm, grad, loss_ref,
            dens, rad, trans, next_out, prev_out, next_in, prev_in,
-           summary, gathered, before, answer, answers, loss_z, loss_sum, loss_d,
-           load_sem, halo_send, halo_recv, sum_send, sum_recv,
-           ans_send, ans_recv, z_send, z_recv, d_send, d_recv):
+           summary, gathered, before, answer, answers, wanted, loss_all,
+           load_sem, target_sem, halo_send, halo_recv, sum_send, sum_recv,
+           ans_send, ans_recv, loss_send, loss_recv):
     slabs, tiles_z, rows, tiles = sizes
     bands = rows // SUB
     share = tiles // slabs
@@ -26,6 +26,18 @@
     plane = rows * tiles
     me = lax.axis_index("depth")
     my_z = lax.axis_index("rays")
+    devices = slabs * tiles_z
+    my_id = me * tiles_z + my_z
+    paired = slabs & (slabs - 1) == 0
+
+    def partner(who, k, back=False):
+        if not paired:
+            return lax.rem(who + (slabs - k if back else k), slabs)
+        found, bit = 0, 1
+        while bit < slabs:
+            found = found + ((who // bit + k // bit) % 2) * bit
+            bit *= 2
+        return found
 
     order = [0] + ([bands - 1] if bands > 1 else []) + list(range(1, bands - 1))
     span = tiles * SUB
@@ -44,6 +56,10 @@
         for copy in load(band):
             copy.start()
 
+    target_copy = pltpu.make_async_copy(
+        target_hbm.at[:, pl.ds(pl.multiple_of(me * share * LANE, LANE), share * LANE)], wanted, target_sem)
+    target_copy.start()
+
     barrier = pltpu.get_barrier_semaphore()
     for k in range(1, slabs):
         pl.semaphore_signal(barrier, inc=1, device_id={"depth": lax.rem(me + k, slabs)}, device_id_type=MESH)
@@ -83,13 +99,8 @@
 
     @pl.when(me > 0)
     def _():
-        for k in range(slabs):
-            halo(0, lax.rem(me + k, slabs)).start()
-
-    @pl.when(me < slabs - 1)
-    def _():
-        for k in range(slabs):
-            halo(1, lax.rem(me + slabs - k, slabs)).start()
+        for k in range(slabs - 1, -1, -1):
+            halo(0, partner(me - 1, k)).start()
 
     @pl.when(me == slabs - 1)
     def _():
@@ -147,16 +158,23 @@
                 summary[p, 1 + c, inner] = color[c]
 
     @pl.loop(1, slabs)
-    def _(k):
-        p = lax.rem(me + k, slabs)
+    def _(i):
+        p = partner(me, slabs - i)
         forward(p)
         send_summary(p).start()
 
+    @pl.when(me < slabs - 1)
+    def _():
+        for k in range(slabs):
+            halo(1, partner(me + 1, k)).start()
+
     forward(me)
     gathered[me] = summary[me]
+    target_copy.wait()
+
     @pl.loop(1, slabs)
     def _(k):
-        recv_summary(lax.rem(me + slabs - k, slabs)).wait_recv()
+        recv_summary(partner(me, k, True)).wait_recv()
 
     start = jnp.zeros((share, LANE), jnp.float32)
     pixel = [jnp.zeros((share, LANE), jnp.float32) for _ in range(CHANNELS)]
@@ -171,11 +189,23 @@
 
     residual, loss = [], jnp.zeros((share, LANE), jnp.float32)
     for c in range(CHANNELS):
-        wanted = jnp.concatenate(
-            [target_ref[c:c + 1, pl.ds(pl.multiple_of((me * share + t) * LANE, LANE), LANE)] for t in range(share)], axis=0)
-        error = pixel[c] - wanted
+        goal = jnp.concatenate(
+            [wanted[c:c + 1, t * LANE:(t + 1) * LANE] for t in range(share)], axis=0)
+        error = pixel[c] - goal
         residual.append(2.0 * error)
         loss = loss + error * error
+
+    loss_all[my_id] = jnp.sum(loss, axis=0, keepdims=True)
+
+    def loss_copy(other, slot):
+        return pltpu.make_async_remote_copy(
+            src_ref=loss_all.at[my_id], dst_ref=loss_all.at[slot],
+            send_sem=loss_send.at[other], recv_sem=loss_recv.at[slot],
+            device_id={"depth": other // tiles_z, "rays": lax.rem(other, tiles_z)}, device_id_type=MESH)
+
+    @pl.loop(1, devices)
+    def _(k):
+        loss_copy(lax.rem(my_id + k, devices), my_id).start()
 
     def send_answer(q):
         return pltpu.make_async_remote_copy(
@@ -189,8 +219,8 @@
             send_sem=ans_send.at[q], recv_sem=ans_recv.at[q],
             device_id={"depth": q}, device_id_type=MESH)
 
-    for k in list(range(1, slabs)) + [0]:
-        q = lax.rem(me + k, slabs)
+    for k in range(slabs - 1, -1, -1):
+        q = partner(me, k)
         behind = residual[0] * (pixel[0] - before[q, 0])
         for c in range(1, CHANNELS):
             behind = behind + residual[c] * (pixel[c] - before[q, c])
@@ -201,23 +231,6 @@
             send_answer(q).start()
         else:
             answers[me] = answer[me]
-
-    loss_z[my_z] = loss
-
-    def z_copy(z, slot):
-        return pltpu.make_async_remote_copy(
-            src_ref=loss_z.at[my_z], dst_ref=loss_z.at[slot],
-            send_sem=z_send.at[z], recv_sem=z_recv.at[slot],
-            device_id={"rays": z}, device_id_type=MESH)
-
-    def d_copy(q, slot):
-        return pltpu.make_async_remote_copy(
-            src_ref=loss_sum, dst_ref=loss_d.at[slot],
-            send_sem=d_send.at[q], recv_sem=d_recv.at[slot],
-            device_id={"depth": q}, device_id_type=MESH)
-
-    for k in range(1, tiles_z):
-        z_copy(lax.rem(my_z + k, tiles_z), my_z).start()
 
     def backward(p):
         @pl.when(me > 0)
@@ -256,37 +269,26 @@
                 grad[pl.ds(base, group, stride=SUB), :] = scale * (a + a_prev) - behind
                 a_prev, v_now = a, v_next
     backward(me)
-    half_way = max(1, slabs // 2)
-
-    @pl.loop(1, half_way)
-    def _(k):
-        p = lax.rem(me + slabs - k, slabs)
+
+    def finish(k):
+        p = partner(me, k, True)
         recv_answer(p).wait_recv()
         backward(p)
 
-    for k in range(1, tiles_z):
-        z = lax.rem(my_z + k, tiles_z)
-        z_copy(z, z).wait_recv()
-    total = loss_z[0]
-    for z in range(1, tiles_z):
-        total = total + loss_z[z]
-    loss_sum[...] = total
-    loss_d[me] = total
-    for k in range(1, slabs):
-        d_copy(lax.rem(me + k, slabs), me).start()
-
-    @pl.loop(half_way, slabs)
+    if slabs > 1:
+        finish(1)
+
+    @pl.loop(1, slabs - 1)
+    def _(i):
+        finish(slabs - i)
+
+    @pl.loop(1, devices)
     def _(k):
-        p = lax.rem(me + slabs - k, slabs)
-        recv_answer(p).wait_recv()
-        backward(p)
-
-    for k in range(1, slabs):
-        q = lax.rem(me + k, slabs)
-        d_copy(q, q).wait_recv()
-    total = loss_d[0]
-    for q in range(1, slabs):
-        total = total + loss_d[q]
+        other = lax.rem(my_id + k, devices)
+        loss_copy(other, other).wait_recv()
+    total = loss_all[0]
+    for other in range(1, devices):
+        total = total + loss_all[other]
     loss_ref[0, 0] = jnp.sum(total) / (float(CHANNELS) * tiles_z * tiles * LANE)
 
     @pl.when(me > 0)
@@ -303,9 +305,10 @@
         q = lax.rem(me + k, slabs)
         send_summary(q).wait_send()
         send_answer(q).wait_send()
-        d_copy(q, me).wait_send()
-    for k in range(1, tiles_z):
-        z_copy(lax.rem(my_z + k, tiles_z), my_z).wait_send()
+
+    @pl.loop(1, devices)
+    def _(k):
+        loss_copy(lax.rem(my_id + k, devices), my_id).wait_send()
 
 
 def flat(x):
@@ -328,7 +331,7 @@
             jax.ShapeDtypeStruct((rows * tiles, LANE), jnp.float32),
             jax.ShapeDtypeStruct((1, 1), jnp.float32),
         ),
-        in_specs=[stay, stay, pl.BlockSpec(memory_space=pltpu.VMEM)],
+        in_specs=[stay, stay, stay],
         out_specs=(pl.BlockSpec(memory_space=pltpu.VMEM), pl.BlockSpec(memory_space=pltpu.SMEM)),
         scratch_shapes=[
             vmem(rows * tiles, LANE),
@@ -343,17 +346,16 @@
             vmem(slabs, CHANNELS, share, LANE),
             vmem(slabs, 2 + CHANNELS, share, LANE),
             vmem(slabs, 2 + CHANNELS, share, LANE),
-            vmem(tiles_z, share, LANE),
-            vmem(share, LANE),
-            vmem(slabs, share, LANE),
-            dma(1 + CHANNELS, bands),
+            vmem(CHANNELS, share * LANE),
+            vmem(slabs * tiles_z, 1, LANE),
+            dma(1 + CHANNELS, bands), pltpu.SemaphoreType.DMA,
             dma(2, slabs), dma(2, slabs),
             dma(slabs), dma(slabs), dma(slabs), dma(slabs),
-            dma(tiles_z), dma(tiles_z), dma(slabs), dma(slabs),
+            dma(slabs * tiles_z), dma(slabs * tiles_z),
         ],
         compiler_params=pltpu.CompilerParams(
-            collective_id=0, has_side_effects=True, vmem_limit_bytes=58 * 1024 * 1024),
-    )(flat(density), flat(radiance), target)
+            collective_id=0, has_side_effects=True, vmem_limit_bytes=50 * 1024 * 1024),
+    )(flat(density), flat(radiance), pltpu.with_memory_space_constraint(target, pltpu.HBM))
     grad = grad.reshape(bands, tiles, SUB, LANE).swapaxes(1, 2).reshape(rows, rays)
     return grad, loss.reshape(())
 

time: 31.1 us -> 26.9 us (0.86)
  Pallas kernels: 25.4 us -> 23.1 us
  local copies, waits for them, and re-layouts: 3.05 us -> 1.32 us
    pallas_call x1, Pallas kernels: 25.4 us -> 23.1 us  [on_device(): pl.pallas_call(functools.partial(kernel, (slabs, tiles_z, rows, tiles)),...]
    unnamed x1, local copies, waits for them, and re-layouts: 3.05 us -> 1.32 us
where the time goes in v2:
time: 26.9 us; the launch traced here: 26.7 us
  Pallas kernels  23.1 us (86%)
  between operations  2.33 us (9%)
  local copies, waits for them, and re-layouts  1.32 us (5%)
    pallas_call x1, Pallas kernels, on_device(): pl.pallas_call(functools.partial(kernel, (slabs, tiles_z, rows, tiles)),...  23.1 us
    unnamed x1, local copies, waits for them, and re-layouts  1.32 us

profile of v2, /device:TPU:0, one launch (start us, length us, event | category | flops | bytes accessed | tf_op | source)
XLA Modules:
  0.0 26.7 jit_solution(10131258970234038507)
XLA Ops:
  0.6 23.1 %shard_map.50 = (f32[4096,128]{1,0:T(8,128)S(1)}, f32[1,1]{1,0:T(1,128)}) custom-call(f32[4096,128]{1,0:T(8,128)} %bitcast.18, f32[12288,128]{1,0:T(8,128)} %bitcast.17, f32[3,16384]{1,0:T(4,128)} %target_hbm.1), custom_call_target="tpu_custom_call" | custom-call | tf_op jit(solution)/shard_map/pallas_call | solution.py:328
  23.7 1.3 %copy.7 = f32[32,16384]{1,0:T(8,128)} copy(f32[32,16384]{1,0:T(8,128)S(1)} %bitcast.16) | data formatting | bytes 4194304

commit v3 on v2

--- a/solution.py
+++ b/solution.py
@@ -39,7 +39,7 @@
             bit *= 2
         return found
 
-    order = [0] + ([bands - 1] if bands > 1 else []) + list(range(1, bands - 1))
+    order = range(bands)
     span = tiles * SUB
 
     def load(band):
@@ -70,9 +70,8 @@
         base = start + ((r // SUB) * tiles + first) * SUB + r % SUB
         return ref[pl.ds(base, count, stride=SUB), :]
 
-    for band in order[:2]:
-        for copy in load(band):
-            copy.wait()
+    for copy in load(0):
+        copy.wait()
 
     @pl.loop(0, tiles // group)
     def _(b):
@@ -82,7 +81,6 @@
         next_out[chunk, 0, inner] = row(dens, 0, first, group, 0)
         for c in range(CHANNELS):
             next_out[chunk, 1 + c, inner] = row(rad, c * plane, first, group, 0)
-            prev_out[chunk, c, inner] = row(rad, c * plane, first, group, rows - 1)
 
     pl.semaphore_wait(barrier, slabs - 1 + tiles_z - 1)
 
@@ -110,7 +108,7 @@
     def _():
         prev_in[...] = jnp.zeros_like(prev_in)
 
-    for band in order[2:]:
+    for band in order[1:]:
         for copy in load(band):
             copy.wait()
 
@@ -125,6 +123,30 @@
             src_ref=summary.at[q], dst_ref=gathered.at[q],
             send_sem=sum_send.at[q], recv_sem=sum_recv.at[q],
             device_id={"depth": q}, device_id_type=MESH)
+
+    @pl.loop(0, tiles // group)
+    def _(b):
+        first = b * group
+        p = first // share
+        inner = pl.ds(first - p * share, group)
+        d_now = row(dens, 0, first, group, 0)
+        c_now = [row(rad, c * plane, first, group, 0) for c in range(CHANNELS)]
+        depth = jnp.zeros((group, LANE), jnp.float32)
+        t_now = jnp.ones((group, LANE), jnp.float32)
+        color = [jnp.zeros((group, LANE), jnp.float32) for _ in range(CHANNELS)]
+        for r in range(rows - 1):
+            d_next = row(dens, 0, first, group, r + 1)
+            c_next = [row(rad, c * plane, first, group, r + 1) for c in range(CHANNELS)]
+            depth = depth + (d_now + d_next)
+            t_next = jnp.exp2(depth * (-HALF_LOG2E))
+            weight = t_now - t_next
+            color = [color[c] + weight * (c_now[c] + c_next[c]) for c in range(CHANNELS)]
+            trans[r, pl.ds(first, group)] = t_next
+            d_now, c_now, t_now = d_next, c_next, t_next
+        summary[p, 0, inner] = depth + d_now
+        for c in range(CHANNELS):
+            summary[p, 1 + c, inner] = color[c]
+            prev_out[p, c, inner] = c_now[c]
 
     def forward(p):
         @pl.when(me < slabs - 1)
@@ -134,28 +156,15 @@
         @pl.loop(0, share // group)
         def _(b):
             inner = pl.ds(b * group, group)
-            first = p * share + b * group
-            d_now = row(dens, 0, first, group, 0)
-            c_now = [row(rad, c * plane, first, group, 0) for c in range(CHANNELS)]
-            depth = jnp.zeros((group, LANE), jnp.float32)
-            t_now = jnp.ones((group, LANE), jnp.float32)
-            color = [jnp.zeros((group, LANE), jnp.float32) for _ in range(CHANNELS)]
-            for r in range(rows):
-                if r + 1 < rows:
-                    d_next = row(dens, 0, first, group, r + 1)
-                    c_next = [row(rad, c * plane, first, group, r + 1) for c in range(CHANNELS)]
-                else:
-                    d_next = next_in[p, 0, inner]
-                    c_next = [next_in[p, 1 + c, inner] for c in range(CHANNELS)]
-                depth = depth + (d_now + d_next)
-                t_next = jnp.exp2(depth * (-HALF_LOG2E))
-                weight = t_now - t_next
-                color = [color[c] + weight * (c_now[c] + c_next[c]) for c in range(CHANNELS)]
-                trans[r, pl.ds(first, group)] = t_next
-                d_now, c_now, t_now = d_next, c_next, t_next
+            here = pl.ds(p * share + b * group, group)
+            depth = summary[p, 0, inner] + next_in[p, 0, inner]
+            t_next = jnp.exp2(depth * (-HALF_LOG2E))
+            weight = trans[rows - 2, here] - t_next
+            trans[rows - 1, here] = t_next
             summary[p, 0, inner] = depth
             for c in range(CHANNELS):
-                summary[p, 1 + c, inner] = color[c]
+                summary[p, 1 + c, inner] = summary[p, 1 + c, inner] + weight * (
+                    prev_out[p, c, inner] + next_in[p, 1 + c, inner])
 
     @pl.loop(1, slabs)
     def _(i):
@@ -197,15 +206,20 @@
 
     loss_all[my_id] = jnp.sum(loss, axis=0, keepdims=True)
 
-    def loss_copy(other, slot):
-        return pltpu.make_async_remote_copy(
-            src_ref=loss_all.at[my_id], dst_ref=loss_all.at[slot],
-            send_sem=loss_send.at[other], recv_sem=loss_recv.at[slot],
-            device_id={"depth": other // tiles_z, "rays": lax.rem(other, tiles_z)}, device_id_type=MESH)
-
-    @pl.loop(1, devices)
-    def _(k):
-        loss_copy(lax.rem(my_id + k, devices), my_id).start()
+    others_z = [lax.rem(my_z + k, tiles_z) for k in range(tiles_z)]
+
+    def loss_copy(piece, depth, z):
+        return pltpu.make_async_remote_copy(
+            src_ref=loss_all.at[piece], dst_ref=loss_all.at[piece],
+            send_sem=loss_send, recv_sem=loss_recv,
+            device_id={"depth": depth, "rays": z}, device_id_type=MESH)
+
+    def send_losses():
+        for k in range(slabs - 1, -1, -1):
+            depth = partner(me, k)
+            for z in others_z[::-1]:
+                if k or z is not others_z[0]:
+                    loss_copy(pl.ds(my_id, 1), depth, z).start()
 
     def send_answer(q):
         return pltpu.make_async_remote_copy(
@@ -229,7 +243,9 @@
             answer[q, 2 + c] = residual[c]
         if k:
             send_answer(q).start()
-        else:
+        if k == max(0, slabs - 2):
+            send_losses()
+        if not k:
             answers[me] = answer[me]
 
     def backward(p):
@@ -282,10 +298,8 @@
     def _(i):
         finish(slabs - i)
 
-    @pl.loop(1, devices)
-    def _(k):
-        other = lax.rem(my_id + k, devices)
-        loss_copy(other, other).wait_recv()
+    every_other = loss_copy(pl.ds(0, devices - 1), me, my_z)
+    every_other.wait_recv()
     total = loss_all[0]
     for other in range(1, devices):
         total = total + loss_all[other]
@@ -306,9 +320,7 @@
         send_summary(q).wait_send()
         send_answer(q).wait_send()
 
-    @pl.loop(1, devices)
-    def _(k):
-        loss_copy(lax.rem(my_id + k, devices), my_id).wait_send()
+    every_other.wait_send()
 
 
 def flat(x):
@@ -351,7 +363,7 @@
             dma(1 + CHANNELS, bands), pltpu.SemaphoreType.DMA,
             dma(2, slabs), dma(2, slabs),
             dma(slabs), dma(slabs), dma(slabs), dma(slabs),
-            dma(slabs * tiles_z), dma(slabs * tiles_z),
+            pltpu.SemaphoreType.DMA, pltpu.SemaphoreType.DMA,
         ],
         compiler_params=pltpu.CompilerParams(
             collective_id=0, has_side_effects=True, vmem_limit_bytes=50 * 1024 * 1024),

time: 26.9 us -> 25.5 us (0.948)
  Pallas kernels: 23.1 us -> 21.7 us
    pallas_call x1, Pallas kernels: 23.1 us -> 21.7 us  [on_device(): pl.pallas_call(functools.partial(kernel, (slabs, tiles_z, rows, tiles)),...]
where the time goes in v3:
time: 25.5 us; the launch traced here: 25.3 us
  Pallas kernels  21.7 us (85%)
  between operations  2.33 us (9%)
  local copies, waits for them, and re-layouts  1.32 us (5%)
    pallas_call x1, Pallas kernels, on_device(): pl.pallas_call(functools.partial(kernel, (slabs, tiles_z, rows, tiles)),...  21.7 us
    unnamed x1, local copies, waits for them, and re-layouts  1.32 us

profile of v3, /device:TPU:0, one launch (start us, length us, event | category | flops | bytes accessed | tf_op | source)
XLA Modules:
  0.0 25.3 jit_solution(4489830420626980768)
XLA Ops:
  0.6 21.7 %shard_map.50 = (f32[4096,128]{1,0:T(8,128)S(1)}, f32[1,1]{1,0:T(1,128)}) custom-call(f32[4096,128]{1,0:T(8,128)} %bitcast.18, f32[12288,128]{1,0:T(8,128)} %bitcast.17, f32[3,16384]{1,0:T(4,128)} %target_hbm.1), custom_call_target="tpu_custom_call" | custom-call | tf_op jit(solution)/shard_map/pallas_call | solution.py:340
  22.3 1.3 %copy.7 = f32[32,16384]{1,0:T(8,128)} copy(f32[32,16384]{1,0:T(8,128)S(1)} %bitcast.16) | data formatting | bytes 4194304
